TPU v7x, 32 devices: a whole 2x2x4 slice. The times are simulated.
32 devices in a mesh: dp: 16 (over z, x, core), mp: 2 (over y).
Axes of the slice: x: 2, y: 2, z: 4, core: 2. Of those that a mesh axis runs over, the one named last changes fastest.
Arguments:
- tokens: bfloat16 [2560, 1024], P('dp', 'mp'), may hold values from -6 to 6
- slot_embed: bfloat16 [2560, 1024], P('dp', 'mp'), may hold values from -0.1875 to 0.1875
- price_units: int32 [2560], P('dp'), may hold values from 0 to 1535
- unassigned: int32 [2560], P('dp'), may hold values from 0 to 1, as said below
Outputs:
- new_prices: float32 [2560], P(('dp', 'mp'))
- margins: float32 [2560], P('dp')
- unassigned_count: int32 [], replicated
Inputs may be any that keep to these rules, and one draw needn't show every extreme that they name: At most 128 of the 160 tokens of each index of dp are unassigned, and some index of dp has exactly 128 in every draw.
All inputs are finite; a program needn't handle non-finite values.
Results may differ from a plain program's by a relative error of at most 0.0004.
Values may be sent and summed in bfloat16 or wider, within the bound.
A program may use at most 128 MiB of HBM per device.

v0:
```python
import jax
import jax.numpy as jnp
from jax import lax
from jax.sharding import PartitionSpec as P

BUSY = 128


unit_price = 1.0 / 512.0


def merged(x, axis, combine):
    everything = jax.tree.map(lambda part: lax.all_gather(part, axis), x)
    first = jax.tree.map(lambda part: part[0], everything)

    def turn(k, so_far):
        return combine(so_far, jax.tree.map(lambda part: part[k], everything))

    return lax.fori_loop(1, lax.axis_size(axis), turn, first)


def top_two(values):
    best_value = jnp.max(values, axis=1)
    where_best = jnp.argmax(values, axis=1)
    column_ids = lax.broadcasted_iota(jnp.int32, values.shape, 1)
    second_value = jnp.max(jnp.where(column_ids == where_best[:, None], -jnp.inf, values), axis=1)
    return (best_value, second_value)


def keep_two(first, later):
    best_first, second_first = first
    best_later, second_later = later
    best_value = jnp.maximum(best_first, best_later)
    second_value = jnp.maximum(
        jnp.minimum(best_first, best_later), jnp.maximum(second_first, second_later)
    )
    return (best_value, second_value)


def compact(mask, busy):
    length = mask.shape[0]
    positions = lax.broadcasted_iota(jnp.int32, (length,), 0)
    ordering = jnp.argsort(jnp.where(mask > 0, positions, positions + length))[:busy]
    return (ordering, mask[ordering] > 0)


def spread_back(ordering, is_valid, margin_rows, length):
    positions = lax.broadcasted_iota(jnp.int32, (ordering.shape[0], length), 1)
    hits = (positions == ordering[:, None]) & is_valid[:, None]
    return jnp.sum(jnp.where(hits, margin_rows[:, None], jnp.float32(0.0)), axis=0)


def excess_of(values, second_value, is_valid):
    excess = jnp.where(is_valid[:, None], values - second_value[:, None], -jnp.inf)
    return jnp.max(excess, axis=0)


def on_device(tokens, slot_embed, price_units, unassigned):
    dp_count = lax.axis_size("dp")
    mp_count = lax.axis_size("mp")
    mp_index = lax.axis_index("mp")
    slot_dev = slot_embed.shape[0]
    half = slot_dev // mp_count
    columns = dp_count * half
    ordering, is_valid = compact(unassigned, BUSY)
    bidders = tokens[ordering]
    own_units = lax.dynamic_slice_in_dim(price_units, mp_index * half, half)
    own_prices = own_units.astype(jnp.float32) * unit_price
    whole_bidders = lax.all_gather(bidders, "mp", axis=1, tiled=True)
    slot_rows_whole = lax.all_to_all(slot_embed, "mp", split_axis=0, concat_axis=1, tiled=True)
    unit_all = jnp.zeros((columns,), jnp.int32)
    slot_rows = lax.all_gather(slot_rows_whole, "dp", axis=0, tiled=True)
    unit_rows = lax.all_gather(own_units, "dp", axis=0, tiled=True)
    block = jnp.einsum("bd,sd->bs", whole_bidders, slot_rows, preferred_element_type=jnp.float32)
    unit_all = lax.dynamic_update_slice_in_dim(unit_all, unit_rows, jnp.int32(0), 0)
    scores, unit_all = (block, unit_all)
    values = scores - (unit_all.astype(jnp.float32) * unit_price)[None, :]
    best_value, second_value = merged(top_two(values), "mp", keep_two)
    terms = excess_of(values, second_value, is_valid).reshape(dp_count, half)
    owner_terms = lax.all_to_all(terms, "dp", split_axis=0, concat_axis=0, tiled=True)
    highest = jnp.max(owner_terms, axis=0)
    new_prices = own_prices + jnp.maximum(highest, jnp.float32(0.0))
    margin_rows = jnp.where(is_valid, best_value - second_value, jnp.float32(0.0))
    margins = spread_back(ordering, is_valid, margin_rows, unassigned.shape[0])
    bidder_total = lax.psum(jnp.sum(unassigned), "dp")
    return (new_prices, margins, bidder_total)


def solution(mesh):
    return jax.shard_map(
        on_device,
        mesh=mesh,
        in_specs=(P("dp", "mp"), P("dp", "mp"), P("dp"), P("dp")),
        out_specs=(P(("dp", "mp")), P("dp"), P()),
        check_vma=False,
    )
```

profile of v0, /device:TPU:0, one launch (start us, length us, event | category | flops | bytes accessed | tf_op | source)
XLA Modules:
  0.0 91.2 jit_solution(4303682870376259929)
XLA Ops:
  7.2 0.0 copy-start
  7.2 0.0 all-gather.7.cloned.1.call-start
  7.2 9.2 %all_to_all.28 = bf16[2,80,512]{2,1,0:T(8,128)(2,1)S(1)} all-to-all(bf16[2,80,512]{2,1,0:T(8,128)(2,1)} %bitcast.19), channel_id=1, replica_groups=mesh['dp'=16,'mp'=2] {'mp'}, dimensions={0} | all-to-all | bytes 327680 | tf_op jit(solution)/shard_map/all_to_all | solution.py:70
  16.4 0.7 copy.12
  17.1 0.0 all-gather.7.cloned.1.call-update
  17.1 1.3 %fusion.6 = (s32[]{:T(128)}, s32[160]{0:T(256)S(1)}) fusion(s32[160]{0:T(256)} %param.7), kind=kLoop, calls=%fused_computation.23 | loop fusion | flops 639 | bytes 1284 | tf_op jit(solution)/shard_map/reduce_sum | solution.py:85
  18.4 3.2 %sort.17 = (s32[160]{0:T(256)}, s32[160]{0:T(256)S(1)}) sort(s32[160]{0:T(256)S(1)} %get-tuple-element.35, s32[160]{0:T(256)S(1)} %iota.27), dimensions={0}, to_apply=%region_0.1 | sort | flops 1280 | bytes 2560 | tf_op jit(solution)/shard_map/jit(argsort)/sort | solution.py:43
  21.6 1.6 %gather_fusion = s32[128]{0:T(128)S(1)} fusion(s32[160]{0:T(256)} %param.7, s32[1024]{0:T(1024)S(1)} %pad_clamp_fusion), kind=kCustom, calls=%fused_computation | custom fusion | bytes 1536 | tf_op jit(solution)/shard_map/gather | solution.py:44
  23.3 0.0 copy-done
  23.3 0.8 gather_fusion.1
  24.1 1.2 %dynamic-slice = u32[1]{0:T(128)} dynamic-slice(u32[32]{0:T(128)} %constant.16, u32[]{:T(128)S(6)} %add.30), dynamic_slice_sizes={1} | dynamic-slice | bytes 12
  26.0 0.9 dynamic-slice_dynamic-update-slice_fusion
  26.9 13.7 %all-reduce.1 = (s32[1280]{0:T(1024)S(1)}, s32[]{:T(128)}) all-reduce(s32[1280]{0:T(1024)S(1)} %dynamic-slice_dynamic-update-slice_fusion, s32[]{:T(128)} %get-tuple-element.34), channel_id=1, replica_groups=mesh['dp'=16,'mp'=2] {'dp'}, use_global_device_ids=true, to_apply=%add | all-reduce | flops 1281 | bytes 10248
  40.6 5.6 %all-gather = bf16[128,1024]{1,0:T(8,128)(2,1)S(1)} all-gather(bf16[128,512]{1,0:T(8,128)(2,1)S(1)} %gather_fusion.1), channel_id=2, replica_groups=mesh['dp'=16,'mp'=2] {'mp'}, dimensions={1}, use_global_device_ids=true | all-gather | bytes 393216 | tf_op jit(solution)/shard_map/all_gather | solution.py:69
  46.2 0.0 copy-start.1
  46.3 14.8 %all-gather.7.cloned.1.call-done = bf16[1280,1024]{1,0:T(8,128)(2,1)} async-done(((bf16[80,1024]{1,0:T(8,128)(2,1)}), bf16[1280,1024]{1,0:T(8,128)(2,1)}) %all-gather.7.cloned.1.call-update) | async-done | bytes 2621456 | tf_op jit(solution)/shard_map/all_gather | solution.py:72
  61.0 2.7 %convolution_subtract_fusion = f32[128,1280]{1,0:T(8,128)S(1)} fusion(bf16[128,1024]{1,0:T(8,128)(2,1)S(1)} %all-gather, bf16[1280,1024]{1,0:T(8,128)(2,1)} %all-gather.7.cloned.1.call-done, f32[1280]{0:T(1024)S(1)} %convert_multiply_fusion), kind=kOutput, calls=%fused_computation.2 | convolution fusion | flops 335708160 | bytes 3544064 | tf_op jit(solution)/shard_map/bd,sd->bs/dot_general | solution.py:74
  63.8 0.4 iota_reduce_fusion
  64.2 4.2 %all-gather.3 = f32[2,1,128]{2,1,0:T(1,128)S(1)} all-gather(f32[1,1,128]{2,1,0:T(1,128)S(1)} %bitcast.21), channel_id=3, replica_groups=mesh['dp'=16,'mp'=2] {'mp'}, dimensions={0}, use_global_device_ids=true | all-gather | bytes 1536 | tf_op jit(solution)/shard_map/all_gather | solution.py:13
  68.4 0.2 select_reduce_fusion.1
  68.6 4.2 %all-gather.4 = f32[2,1,128]{2,1,0:T(1,128)S(1)} all-gather(f32[1,1,128]{2,1,0:T(1,128)S(1)} %bitcast.22), channel_id=4, replica_groups=mesh['dp'=16,'mp'=2] {'mp'}, dimensions={0}, use_global_device_ids=true | all-gather | bytes 1536 | tf_op jit(solution)/shard_map/all_gather | solution.py:13
  72.9 0.1 select_reduce_fusion
  73.0 0.7 all_to_all.24
  73.7 3.6 %all-to-all-start.1 = ((f32[16,1,80]{2,1,0:T(1,128)}), f32[16,1,80]{2,1,0:T(1,128)S(1)}, u32[]{:S(2)}, u32[]{:S(2)}) async-start(f32[16,1,80]{2,1,0:T(1,128)} %all_to_all.24), calls=%async_computation.1 | async-start | bytes 16384 | tf_op jit(solution)/shard_map/all_to_all | solution.py:80
  77.3 0.7 select_reduce_fusion.2
  77.9 5.8 %all-to-all-done.1 = f32[16,1,80]{2,1,0:T(1,128)S(1)} async-done(((f32[16,1,80]{2,1,0:T(1,128)}), f32[16,1,80]{2,1,0:T(1,128)S(1)}, u32[]{:S(2)}, u32[]{:S(2)}) %all-to-all-start.1) | async-done | bytes 5152 | tf_op jit(solution)/shard_map/all_to_all | solution.py:80
  83.7 0.0 copy-done.1
  83.7 0.6 maximum_add_fusion
  (8 shorter events, 0.1 us)
Async XLA Ops:
  7.2 16.1 %copy-start = (bf16[160,512]{1,0:T(8,128)(2,1)S(1)}, bf16[160,512]{1,0:T(8,128)(2,1)}, u32[]{:S(2)}) copy-start(bf16[160,512]{1,0:T(8,128)(2,1)} %param.4) | copy-start | bytes 491524
  7.2 53.9 %all-gather.7.cloned.1.call-start = ((), (), s32[]{:S(2)}) async-start(), calls=%async_computation.2 | async-start | bytes 2785280 | tf_op jit(solution)/shard_map/all_gather | solution.py:72
  46.2 37.5 %copy-start.1 = (s32[160]{0:T(256)S(1)}, s32[160]{0:T(256)}, u32[]{:S(2)}) copy-start(s32[160]{0:T(256)} %param.6) | copy-start | bytes 1924
  73.7 10.0 %all-to-all-start.1 = ((f32[16,1,80]{2,1,0:T(1,128)}), f32[16,1,80]{2,1,0:T(1,128)S(1)}, u32[]{:S(2)}, u32[]{:S(2)}) async-start(f32[16,1,80]{2,1,0:T(1,128)} %all_to_all.24), calls=%async_computation.1 | async-start | bytes 16384 | tf_op jit(solution)/shard_map/all_to_all | solution.py:80
Sparse Core Ops, SparseCore 0:
  17.2 43.7 all-gather.6
where the time goes:
time: 91.5 us; the launch traced here: 91.2 us
  blocking collectives  37 us (40%)
  waiting for transfers between devices  20.6 us (23%)
  between operations  14.7 us (16%)
  other arithmetic  6.56 us (7%)
  local copies, waits for them, and re-layouts  5.97 us (7%)
  starting transfers between devices  3.59 us (4%)
  matrix products  2.73 us (3%)
    all_gather x1, waiting for transfers between devices, on_device(): slot_rows = lax.all_gather(slot_rows_whole, 'dp', axis=0, tiled=True)  14.8 us
    unnamed x1, blocking collectives  13.7 us
    all_to_all x1, blocking collectives, on_device(): lax.all_to_all(slot_embed, 'mp', split_axis=0, concat_axis=1, tiled=True)  9.2 us
    all_gather x2, blocking collectives, merged(): everything = jax.tree.map(lambda part: lax.all_gather(part, axis), x)  8.47 us
    all_to_all x1, waiting for transfers between devices, on_device(): lax.all_to_all(terms, 'dp', split_axis=0, concat_axis=0, tiled=True)  5.75 us
    all_gather x1, blocking collectives, on_device(): whole_bidders = lax.all_gather(bidders, 'mp', axis=1, tiled=True)  5.62 us
    all_to_all x1, starting transfers between devices, on_device(): lax.all_to_all(terms, 'dp', split_axis=0, concat_axis=0, tiled=True)  3.55 us
    sort x1, other arithmetic, compact(): jnp.argsort(jnp.where(mask > 0, positions, positions + length))[:busy]  3.17 us
  transfers between devices with their start and end apart: 2, of which 2 were waited for; matrix products, arithmetic and copies ran while one was open for 11% of the time, Pallas kernels for 0%

commit v1 on v0

v1 whole, which is shorter than its diff:
```python
import functools

import jax
import jax.numpy as jnp
from jax import lax
from jax.experimental import pallas as pl
from jax.experimental.pallas import tpu as pltpu
from jax.sharding import PartitionSpec as P

MESH = pl.DeviceIdType.MESH
GROUP = 4
LANES = 128

unit_price = 1.0 / 512.0


def loop(low, high, body):
    if high - low <= 8:
        for k in range(low, high):
            body(k)
    else:
        lax.fori_loop(low, high, lambda k, carry: (body(k), carry)[1], 0)


def kernel(
    lines, tok_in, slot_in, price_in, mask_in, prices_out, margins_out, count_out,
    tok, slots, spare, prices, masks, stats, raises, outgoing, vals, best, second,
    load_sem, tok_send, tok_recv, swap_send, right_send, left_send, slot_recv,
    price_send, price_recv, mask_send, mask_recv, stat_send, stat_recv, raise_send, raise_recv,
):
    dp = lax.axis_index("dp")
    y = lax.axis_index("mp")
    yo = 1 - y
    i, z = lax.rem(dp, GROUP), lax.div(dp, GROUP)
    i1 = i + 1 - 2 * lax.rem(i, 2)
    i2 = lax.rem(i + 2, GROUP)
    i3 = GROUP - 1 - i
    half = slots.shape[2]
    own = tok.shape[2]

    def at(ii, zz, yy):
        return {"dp": zz * GROUP + ii, "mp": yy}

    def send(src, dst, send_sem, recv_sem, device):
        return pltpu.make_async_remote_copy(
            src_ref=src, dst_ref=dst, send_sem=send_sem, recv_sem=recv_sem,
            device_id=device, device_id_type=MESH,
        )

    def arrived(dst, recv_sem):
        send(dst, dst, tok_send.at[0], recv_sem, at(i1, z, y)).wait_recv()

    loads = [
        pltpu.make_async_copy(slot_in.at[y], slots.at[y, z], load_sem.at[0]),
        pltpu.make_async_copy(slot_in.at[yo], spare, load_sem.at[1]),
        pltpu.make_async_copy(tok_in, tok.at[y, i], load_sem.at[2]),
        pltpu.make_async_copy(price_in, prices.at[z], load_sem.at[3]),
        pltpu.make_async_copy(mask_in, masks.at[i], load_sem.at[4]),
    ]
    for load in loads:
        load.start()

    plane = [(i1, y), (i2, y), (i3, y), (i, yo), (i1, yo), (i2, yo), (i3, yo)]
    barrier = pltpu.get_barrier_semaphore()
    for ii, yy in plane:
        pl.semaphore_signal(barrier, inc=1, device_id=at(ii, z, yy), device_id_type=MESH)

    def greet(d):
        pl.semaphore_signal(
            barrier, inc=1, device_id=at(i, lax.rem(z + d, lines), y), device_id_type=MESH
        )

    loop(1, lines, greet)
    pl.semaphore_wait(barrier, len(plane) + lines - 1)

    has_right, has_left = z < lines - 1, z > 0

    def to_right(f, zb):
        return send(slots.at[f, zb], slots.at[f, zb], right_send.at[f, zb], slot_recv.at[f, zb],
                    at(i, lax.rem(z + 1, lines), y))

    def to_left(f, zb):
        return send(slots.at[f, zb], slots.at[f, zb], left_send.at[f, zb], slot_recv.at[f, zb],
                    at(i, lax.rem(z + lines - 1, lines), y))

    def send_both(f):
        @pl.when(has_right)
        def _():
            to_right(f, z).start()

        @pl.when(has_left)
        def _():
            to_left(f, z).start()

    loads[0].wait()
    send_both(y)
    loads[1].wait()
    swap = send(spare, slots.at[y, z], swap_send, slot_recv.at[y, z], at(i, z, yo))
    swap.start()
    loads[2].wait()
    mine = tok.at[y, i]
    token_sends = [
        send(mine, mine, tok_send.at[k], tok_recv.at[y, i], device)
        for k, device in enumerate([at(i2, z, y), at(i, z, yo), at(i1, z, y), at(i2, z, yo)])
    ]
    for copy in token_sends:
        copy.start()
    loads[3].wait()
    loads[4].wait()

    def send_price(d):
        send(prices.at[z], prices.at[z], price_send.at[d], price_recv.at[z],
             at(i, lax.rem(z + d, lines), y)).start()

    loop(1, lines, send_price)
    mask_sends = [
        send(masks.at[i], masks.at[i], mask_send.at[k], mask_recv.at[i], at(ii, z, y))
        for k, ii in enumerate([i1, i2, i3])
    ]
    for copy in mask_sends:
        copy.start()

    def relay(d, f):
        @pl.when(has_right & (z - d >= 0))
        def _():
            zb = lax.max(z - d, 0)
            arrived(slots.at[f, zb], slot_recv.at[f, zb])
            to_right(f, zb).start()

        @pl.when(has_left & (z + d < lines))
        def _():
            zb = lax.min(z + d, lines - 1)
            arrived(slots.at[f, zb], slot_recv.at[f, zb])
            to_left(f, zb).start()

    def pass_on(f, ii, k):
        block = tok.at[f, ii]
        arrived(block, tok_recv.at[f, ii])
        copy = send(block, block, tok_send.at[k], tok_recv.at[f, ii], at(i1, z, y))
        copy.start()
        token_sends.append(copy)

    relay(1, y)
    arrived(slots.at[yo, z], slot_recv.at[yo, z])
    send_both(yo)
    pass_on(y, i2, 4)
    relay(1, yo)
    pass_on(yo, i, 5)
    if lines > 2:
        def relay_both(d):
            relay(d, y)
            relay(d, yo)

        loop(2, lines - 1, relay_both)
    pass_on(yo, i2, 6)
    for f, ii in [(y, i1), (y, i3), (yo, i1), (yo, i3)]:
        arrived(tok.at[f, ii], tok_recv.at[f, ii])

    def price_arrived(d):
        zb = lax.rem(z + d, lines)
        arrived(prices.at[zb], price_recv.at[zb])

    loop(1, lines, price_arrived)
    for ii in (i1, i2, i3):
        arrived(masks.at[ii], mask_recv.at[ii])

    best[...] = jnp.full_like(best, -jnp.inf)
    second[...] = jnp.full_like(second, -jnp.inf)

    def price_column(zb):
        row = prices[zb].astype(jnp.float32) * unit_price
        shape = (half, row.shape[1])
        hit = lax.broadcasted_iota(jnp.int32, shape, 1) == lax.broadcasted_iota(jnp.int32, shape, 0) + y * half
        return jnp.sum(jnp.where(hit, row, 0.0), axis=1, keepdims=True)

    def score(zb):
        total = None
        for f in range(2):
            bidders = tok[f].reshape(GROUP * own, tok.shape[3])
            part = lax.dot_general(
                slots[f, zb], bidders, (((1,), (1,)), ((), ())), preferred_element_type=jnp.float32
            )
            total = part if total is None else total + part
        v = total - price_column(zb)
        vals[zb] = v
        b, s = best[...], second[...]
        for k in range(half // 8):
            row = v[8 * k:8 * k + 8]
            s = jnp.maximum(s, jnp.minimum(b, row))
            b = jnp.maximum(b, row)
        best[...] = b
        second[...] = s

    score(z)

    def score_at(d):
        @pl.when(z - d >= 0)
        def _():
            zb = lax.max(z - d, 0)

            @pl.when(jnp.logical_not(has_right))
            def _():
                arrived(slots.at[y, zb], slot_recv.at[y, zb])
                arrived(slots.at[yo, zb], slot_recv.at[yo, zb])

            score(zb)

        @pl.when(z + d < lines)
        def _():
            zb = lax.min(z + d, lines - 1)

            @pl.when(jnp.logical_not(has_left))
            def _():
                arrived(slots.at[y, zb], slot_recv.at[y, zb])
                arrived(slots.at[yo, zb], slot_recv.at[yo, zb])

            score(zb)

    loop(1, lines, score_at)

    b, s = best[...], second[...]
    for shift in (4, 2, 1):
        b2, s2 = pltpu.roll(b, shift, 0), pltpu.roll(s, shift, 0)
        s = jnp.maximum(jnp.minimum(b, b2), jnp.maximum(s, s2))
        b = jnp.maximum(b, b2)
    here = y * GROUP + i
    stats[here, 0:1] = b[0:1]
    stats[here, 1:2] = s[0:1]
    stat_sends = [
        send(stats.at[here], stats.at[here], stat_send.at[k], stat_recv.at[here], at(ii, z, yy))
        for k, (ii, yy) in enumerate(plane)
    ]
    for copy in stat_sends:
        copy.start()

    mask = jnp.concatenate([masks[k] for k in range(GROUP)], axis=1)
    bidders_here = jnp.sum(mask.astype(jnp.float32), axis=1, keepdims=True)

    for ii, yy in plane:
        arrived(stats.at[yy * GROUP + ii], stat_recv.at[yy * GROUP + ii])
    b, s = stats[0, 0:1], stats[0, 1:2]
    for k in range(1, 2 * GROUP):
        b2, s2 = stats[k, 0:1], stats[k, 1:2]
        s = jnp.maximum(jnp.minimum(b, b2), jnp.maximum(s, s2))
        b = jnp.maximum(b, b2)
    bar = jnp.where(mask > 0, s, jnp.inf)

    def excess(d):
        zb = lax.rem(z + d, lines)
        column = jnp.max(vals[zb] - bar, axis=1, keepdims=True)
        shape = (half, LANES)
        hit = lax.broadcasted_iota(jnp.int32, shape, 1) == lax.broadcasted_iota(jnp.int32, shape, 0)
        row = jnp.max(jnp.where(hit, column, -jnp.inf), axis=0, keepdims=True)
        row = jnp.where(lax.broadcasted_iota(jnp.int32, row.shape, 1) == LANES - 1, bidders_here, row)
        return zb, row

    def send_excess(d):
        zb, row = excess(d)
        outgoing[zb] = row
        send(outgoing.at[zb], raises.at[z], raise_send.at[d], raise_recv.at[z], at(i, zb, y)).start()

    loop(1, lines, send_excess)
    raises[z] = excess(0)[1]

    margin = jnp.where(mask > 0, b - s, 0.0)
    mine = margin[:, :own]
    for k in range(1, GROUP):
        mine = jnp.where(i == k, margin[:, k * own:(k + 1) * own], mine)
    margins_out[...] = mine
    units = prices[z].astype(jnp.float32)
    own_prices = jnp.where(y == 0, units[:, :half], units[:, half:2 * half]) * unit_price

    def raise_arrived(d):
        zb = lax.rem(z + d, lines)
        arrived(raises.at[zb], raise_recv.at[zb])

    loop(1, lines, raise_arrived)
    highest, total = raises[0], raises[0]
    for k in range(1, lines):
        highest = jnp.maximum(highest, raises[k])
        total = total + raises[k]
    prices_out[...] = own_prices + jnp.maximum(highest[:, :half], 0.0)
    count_out[...] = total[:, LANES - 1:].astype(jnp.int32)

    swap.wait_send()
    for copy in token_sends + mask_sends + stat_sends:
        copy.wait_send()

    def sent(d):
        zb = lax.rem(z + d, lines)
        send(prices.at[z], prices.at[z], price_send.at[d], price_recv.at[z], at(i, zb, y)).wait_send()
        send(outgoing.at[zb], raises.at[z], raise_send.at[d], raise_recv.at[z], at(i, zb, y)).wait_send()

    loop(1, lines, sent)

    def passed(zb):
        @pl.when(has_right & (zb <= z))
        def _():
            to_right(0, zb).wait_send()
            to_right(1, zb).wait_send()

        @pl.when(has_left & (zb >= z))
        def _():
            to_left(0, zb).wait_send()
            to_left(1, zb).wait_send()

    loop(0, lines, passed)


def on_device(tokens, slot_embed, price_units, unassigned):
    lines = lax.axis_size("dp") // GROUP
    own, width = tokens.shape
    slot_dev = slot_embed.shape[0]
    half = slot_dev // 2
    bidders = GROUP * own
    any_ = pl.BlockSpec(memory_space=pl.ANY)
    vmem = pl.BlockSpec(memory_space=pltpu.VMEM)
    dma = pltpu.SemaphoreType.DMA
    new_prices, margins, total = pl.pallas_call(
        functools.partial(kernel, lines),
        out_shape=(
            jax.ShapeDtypeStruct((1, half), jnp.float32),
            jax.ShapeDtypeStruct((1, own), jnp.float32),
            jax.ShapeDtypeStruct((1, 1), jnp.int32),
        ),
        in_specs=[any_] * 4,
        out_specs=(vmem,) * 3,
        scratch_shapes=[
            pltpu.VMEM((2, GROUP, own, width), jnp.bfloat16),
            pltpu.VMEM((2, lines, half, width), jnp.bfloat16),
            pltpu.VMEM((half, width), jnp.bfloat16),
            pltpu.VMEM((lines, 1, slot_dev), jnp.int32),
            pltpu.VMEM((GROUP, 1, own), jnp.int32),
            pltpu.VMEM((2 * GROUP, 2, bidders), jnp.float32),
            pltpu.VMEM((lines, 1, LANES), jnp.float32),
            pltpu.VMEM((lines, 1, LANES), jnp.float32),
            pltpu.VMEM((lines, half, bidders), jnp.float32),
            pltpu.VMEM((8, bidders), jnp.float32),
            pltpu.VMEM((8, bidders), jnp.float32),
            dma((5,)), dma((7,)), dma((2, GROUP)), dma, dma((2, lines)), dma((2, lines)), dma((2, lines)),
            dma((lines,)), dma((lines,)), dma((3,)), dma((GROUP,)), dma((7,)), dma((2 * GROUP,)),
            dma((lines,)), dma((lines,)),
        ],
        compiler_params=pltpu.CompilerParams(collective_id=0, has_side_effects=True),
        name="auction",
    )(tokens, slot_embed.reshape(2, half, width), price_units.reshape(1, -1), unassigned.reshape(1, -1))
    return new_prices.reshape(-1), margins.reshape(-1), total.reshape(())


def solution(mesh):
    return jax.shard_map(
        on_device,
        mesh=mesh,
        in_specs=(P("dp", "mp"), P("dp", "mp"), P("dp"), P("dp")),
        out_specs=(P(("dp", "mp")), P("dp"), P()),
        check_vma=False,
    )
```

time: 91.5 us -> 34.3 us (0.37)
  blocking collectives: 37 us -> 0 us
  Pallas kernels: 0 us -> 29.8 us
  waiting for transfers between devices: 20.6 us -> 0 us
  between operations: 14.7 us -> 2.4 us
  other arithmetic: 6.56 us -> 0 us
  local copies, waits for them, and re-layouts: 5.97 us -> 1.86 us
  starting transfers between devices: 3.59 us -> 0 us
  matrix products: 2.73 us -> 0 us
    pallas_call x0 -> x1, Pallas kernels: none -> 29.8 us  [on_device(): pl.pallas_call(functools.partial(kernel, lines), out_shape=(jax.ShapeDtyp...]
    all_gather x1 -> x0, waiting for transfers between devices: 14.8 us -> none  [on_device(): slot_rows = lax.all_gather(slot_rows_whole, 'dp', axis=0, tiled=True)]
    all_gather x3 -> x0, blocking collectives: 14.1 us -> none  [the longest x2 8.47 us: merged(): everything = jax.tree.map(lambda part: lax.all_gather(part, axis), x)]
    unnamed x1 -> x0, blocking collectives: 13.7 us -> none
    all_to_all x1 -> x0, blocking collectives: 9.2 us -> none  [on_device(): lax.all_to_all(slot_embed, 'mp', split_axis=0, concat_axis=1, tiled=True)]
    all_to_all x1 -> x0, waiting for transfers between devices: 5.75 us -> none  [on_device(): lax.all_to_all(terms, 'dp', split_axis=0, concat_axis=0, tiled=True)]
    all_to_all x1 -> x0, starting transfers between devices: 3.55 us -> none  [on_device(): lax.all_to_all(terms, 'dp', split_axis=0, concat_axis=0, tiled=True)]
    sort x1 -> x0, other arithmetic: 3.17 us -> none  [compact(): jnp.argsort(jnp.where(mask > 0, positions, positions + length))[:busy]]
  transfers between devices with their start and end apart: 2 -> 0, of which waited for: 2 -> 0; matrix products, arithmetic and copies ran while one was open for 11% -> 0% of each run, Pallas kernels for 0% -> 0%
where the time goes in v1:
time: 34.3 us; the launch traced here: 34.1 us
  Pallas kernels  29.8 us (87%)
  between operations  2.4 us (7%)
  local copies, waits for them, and re-layouts  1.86 us (5%)
    pallas_call x1, Pallas kernels, on_device(): pl.pallas_call(functools.partial(kernel, lines), out_shape=(jax.ShapeDtyp...  29.8 us
    unnamed x6, local copies, waits for them, and re-layouts  1.86 us

profile of v1, /device:TPU:0, one launch (start us, length us, event | category | flops | bytes accessed | tf_op | source)
XLA Modules:
  0.0 34.1 jit_solution(3980289984457018204)
XLA Ops:
  0.6 29.8 %auction.1 = (f32[1,80]{1,0:T(1,128)}, f32[1,160]{1,0:T(1,128)}, s32[1,1]{1,0:T(1,128)}) custom-call(bf16[160,512]{1,0:T(8,128)(2,1)} %tok_in.1, bf16[2,80,512]{2,1,0:T(8,128)(2,1)} %bitcast.6, s32[1,160]{1,0:T(1,128)} %bitcast.7, s32[1,160]{1,0:T(1,128)} %bitcast.8), custom_call_target="tpu_custom_call" | custom-call | tf_op jit(solution)/shard_map/auction/pallas_call | solution.py:319
  30.5 0.0 copy-start.1
  30.5 0.6 %copy-done.1 = f32[1,80]{1,0:T(1,128)S(1)} copy-done((f32[1,80]{1,0:T(1,128)S(1)}, f32[1,80]{1,0:T(1,128)}, u32[]{:S(2)}) %copy-start.1) | copy-done | bytes 344
  31.1 0.0 copy-start
  31.1 0.5 %copy.10 = f32[80]{0:T(128)} copy(f32[80]{0:T(128)S(1)} %bitcast.10) | data formatting | bytes 640
  31.6 0.2 copy-done
  31.8 0.6 %copy.11 = f32[160]{0:T(256)} copy(f32[160]{0:T(256)S(1)} %bitcast.9) | data formatting | bytes 1280
Async XLA Ops:
  30.5 0.6 %copy-start.1 = (f32[1,80]{1,0:T(1,128)S(1)}, f32[1,80]{1,0:T(1,128)}, u32[]{:S(2)}) copy-start(f32[1,80]{1,0:T(1,128)} %get-tuple-element.6) | copy-start | bytes 964
  31.1 0.7 %copy-start = (f32[1,160]{1,0:T(1,128)S(1)}, f32[1,160]{1,0:T(1,128)}, u32[]{:S(2)}) copy-start(f32[1,160]{1,0:T(1,128)} %get-tuple-element.7) | copy-start | bytes 1924

commit v2 on v1

v2 whole, which is shorter than its diff:
```python
import functools

import jax
import jax.numpy as jnp
from jax import lax
from jax.experimental import pallas as pl
from jax.experimental.pallas import tpu as pltpu
from jax.sharding import PartitionSpec as P

MESH = pl.DeviceIdType.MESH
BUSY = 128
GROUP = 4
LANES = 128

unit_price = 1.0 / 512.0


def loop(low, high, body):
    if high - low <= 8:
        for k in range(low, high):
            body(k)
    else:
        lax.fori_loop(low, high, lambda k, carry: (body(k), carry)[1], 0)


def iota(shape, axis):
    return lax.broadcasted_iota(jnp.int32, shape, axis)


def column_of(row, size):
    shape = (size, row.shape[1])
    return jnp.sum(jnp.where(iota(shape, 1) == iota(shape, 0), row, 0.0), axis=1, keepdims=True)


def keep_two(first, later):
    b, s = first
    b2, s2 = later
    return jnp.maximum(b, b2), jnp.maximum(jnp.minimum(b, b2), jnp.maximum(s, s2))


def kernel(
    lines, cap, tok_in, slot_in, price_in, mask_in, prices_out, margins_out, count_out,
    slot, toks, raw, spare, prices, masks, where_to, cost, stats, raises, outgoing, vals, gaps, halves,
    load_sem, slot_send, slot_recv, swap_send, right_send, left_send, tok_recv,
    price_send, price_recv, stat_send, stat_recv, raise_send, raise_recv, gap_send, gap_recv,
):
    dp = lax.axis_index("dp")
    y = lax.axis_index("mp")
    yo = 1 - y
    i, z = lax.rem(dp, GROUP), lax.div(dp, GROUP)
    i1 = i + 1 - 2 * lax.rem(i, 2)
    i2 = lax.rem(i + 2, GROUP)
    i3 = GROUP - 1 - i
    own = slot.shape[2]
    half = own // 2
    here = y * GROUP + i

    def at(ii, zz, yy):
        return {"dp": zz * GROUP + ii, "mp": yy}

    def send(src, dst, send_sem, recv_sem, device):
        return pltpu.make_async_remote_copy(
            src_ref=src, dst_ref=dst, send_sem=send_sem, recv_sem=recv_sem,
            device_id=device, device_id_type=MESH,
        )

    def arrived(dst, recv_sem):
        send(dst, dst, slot_send.at[0], recv_sem, at(i1, z, y)).wait_recv()

    loads = [
        pltpu.make_async_copy(mask_in, masks, load_sem.at[0]),
        pltpu.make_async_copy(tok_in, raw, load_sem.at[1]),
        pltpu.make_async_copy(slot_in, slot.at[y, i], load_sem.at[2]),
        pltpu.make_async_copy(price_in, prices.at[i], load_sem.at[3]),
    ]
    for load in loads:
        load.start()

    has_right, has_left = z < lines - 1, z > 0
    plane = [(i1, y), (i2, y), (i3, y), (i, yo), (i1, yo), (i2, yo), (i3, yo)]
    barrier = pltpu.get_barrier_semaphore()
    for ii, yy in plane:
        pl.semaphore_signal(barrier, inc=1, device_id=at(ii, z, yy), device_id_type=MESH)

    @pl.when(has_right)
    def _():
        pl.semaphore_signal(barrier, inc=1, device_id=at(i, z + 1, y), device_id_type=MESH)

    @pl.when(has_left)
    def _():
        pl.semaphore_signal(barrier, inc=1, device_id=at(i, z - 1, y), device_id_type=MESH)

    loads[0].wait()
    live = masks[...] > 0
    ones = jnp.broadcast_to(jnp.where(live, 1.0, 0.0), (8, own)).astype(jnp.bfloat16)
    before = jnp.where(iota((own, own), 0) < iota((own, own), 1), 1.0, 0.0).astype(jnp.bfloat16)
    place = jnp.dot(ones, before, preferred_element_type=jnp.float32)[0:1]
    place = jnp.where(live, place, -1.0)
    where_to[...] = place
    busy = jnp.sum(jnp.where(live, 1.0, 0.0), axis=1, keepdims=True)
    hits = place == iota((2 * cap, own), 0).astype(jnp.float32)
    hits = jnp.where(hits, 1.0, 0.0).astype(jnp.bfloat16)
    loads[1].wait()
    packed = jnp.dot(hits, raw[...], preferred_element_type=jnp.float32).astype(jnp.bfloat16)
    low, high = packed[:cap], packed[cap:]
    toks[y, z] = jnp.where(y == 0, low, high)
    spare[...] = jnp.where(y == 0, high, low)

    @pl.when(has_right & has_left)
    def _():
        pl.semaphore_wait(barrier, len(plane) + 2)

    @pl.when(jnp.logical_not(has_right & has_left))
    def _():
        pl.semaphore_wait(barrier, len(plane) + min(lines - 1, 1))

    def to_right(f, zb):
        return send(toks.at[f, zb], toks.at[f, zb], right_send.at[f, zb], tok_recv.at[f, zb],
                    at(i, lax.rem(z + 1, lines), y))

    def to_left(f, zb):
        return send(toks.at[f, zb], toks.at[f, zb], left_send.at[f, zb], tok_recv.at[f, zb],
                    at(i, lax.rem(z + lines - 1, lines), y))

    def send_both(f):
        @pl.when(has_right)
        def _():
            to_right(f, z).start()

        @pl.when(has_left)
        def _():
            to_left(f, z).start()

    swap = send(spare, toks.at[y, z], swap_send, tok_recv.at[y, z], at(i, z, yo))
    swap.start()
    send_both(y)
    loads[2].wait()
    mine = slot.at[y, i]
    slot_sends = [
        send(mine, mine, slot_send.at[k], slot_recv.at[y, i], device)
        for k, device in enumerate([at(i2, z, y), at(i, z, yo), at(i1, z, y), at(i2, z, yo)])
    ]
    for copy in slot_sends:
        copy.start()
    loads[3].wait()
    price_sends = [
        send(prices.at[i], prices.at[i], price_send.at[k], price_recv.at[i], at(ii, z, y))
        for k, ii in enumerate([i1, i2, i3])
    ]
    for copy in price_sends:
        copy.start()

    def relay(d, f):
        @pl.when(has_right & (z - d >= 0))
        def _():
            zb = lax.max(z - d, 0)
            arrived(toks.at[f, zb], tok_recv.at[f, zb])
            to_right(f, zb).start()

        @pl.when(has_left & (z + d < lines))
        def _():
            zb = lax.min(z + d, lines - 1)
            arrived(toks.at[f, zb], tok_recv.at[f, zb])
            to_left(f, zb).start()

    def pass_on(f, ii, k):
        block = slot.at[f, ii]
        arrived(block, slot_recv.at[f, ii])
        copy = send(block, block, slot_send.at[k], slot_recv.at[f, ii], at(i1, z, y))
        copy.start()
        slot_sends.append(copy)

    arrived(toks.at[yo, z], tok_recv.at[yo, z])
    send_both(yo)
    relay(1, y)
    pass_on(y, i2, 4)
    relay(1, yo)
    pass_on(yo, i, 5)
    if lines > 2:
        def relay_both(d):
            relay(d, y)
            relay(d, yo)

        loop(2, lines - 1, relay_both)
    for ii in (i1, i2, i3):
        arrived(prices.at[ii], price_recv.at[ii])
    for k in range(GROUP):
        column = column_of(prices[k].astype(jnp.float32) * unit_price, own)
        cost[k * own:(k + 1) * own] = jnp.broadcast_to(column, (own, cap))
    pass_on(yo, i2, 6)
    for f, ii in [(y, i1), (y, i3), (yo, i1), (yo, i3)]:
        arrived(slot.at[f, ii], slot_recv.at[f, ii])

    def score(zb):
        total = None
        for f in range(2):
            rows = slot[f].reshape(GROUP * own, slot.shape[3])
            part = lax.dot_general(
                rows, toks[f, zb], (((1,), (1,)), ((), ())), preferred_element_type=jnp.float32
            )
            total = part if total is None else total + part
        v = total - cost[...]
        vals[zb] = v
        step = 32
        b, s = v[:step], jnp.full((step, cap), -jnp.inf)
        for k in range(1, GROUP * own // step):
            row = v[step * k:step * (k + 1)]
            s = jnp.maximum(s, jnp.minimum(b, row))
            b = jnp.maximum(b, row)
        while step > 8:
            step //= 2
            b, s = keep_two((b[:step], s[:step]), (b[step:], s[step:]))
        for shift in (4, 2, 1):
            b, s = keep_two((b, s), (pltpu.roll(b, shift, 0), pltpu.roll(s, shift, 0)))
        stats[z, pl.ds(zb, 1)] = jnp.concatenate([b[0:1], s[0:1]], axis=1)

    score(z)

    def score_at(d):
        @pl.when(z - d >= 0)
        def _():
            zb = lax.max(z - d, 0)

            @pl.when(jnp.logical_not(has_right))
            def _():
                arrived(toks.at[y, zb], tok_recv.at[y, zb])
                arrived(toks.at[yo, zb], tok_recv.at[yo, zb])

            score(zb)

        @pl.when(z + d < lines)
        def _():
            zb = lax.min(z + d, lines - 1)

            @pl.when(jnp.logical_not(has_left))
            def _():
                arrived(toks.at[y, zb], tok_recv.at[y, zb])
                arrived(toks.at[yo, zb], tok_recv.at[yo, zb])

            score(zb)

    stats[z, lines:] = jnp.broadcast_to(busy, (lines, LANES))
    loop(1, lines, score_at)

    def stat_to(d):
        return send(stats.at[z], stats.at[z], stat_send.at[d], stat_recv.at[z], at(i, lax.rem(z + d, lines), y))

    loop(1, lines, lambda d: stat_to(d).start())

    def stat_arrived(d):
        zb = lax.rem(z + d, lines)
        arrived(stats.at[zb], stat_recv.at[zb])

    loop(1, lines, stat_arrived)
    b, s = stats[0, :lines, :cap], stats[0, :lines, cap:]
    for k in range(1, lines):
        b, s = keep_two((b, s), (stats[k, :lines, :cap], stats[k, :lines, cap:]))
    number = y * cap + iota((1, cap), 1)
    top, bidders = None, None
    for k in range(lines):
        count = stats[k, lines:lines + 1, :cap]
        valid = number.astype(jnp.float32) < count
        gaps[k] = jnp.where(valid, b[k:k + 1] - s[k:k + 1], 0.0)
        excess = vals[k] - jnp.where(valid, s[k:k + 1], jnp.inf)
        top = excess if top is None else jnp.maximum(top, excess)
        bidders = count if bidders is None else bidders + count
    bidders = bidders[:, :1]
    halves[y] = gaps[z]
    gap_to = send(halves.at[y], halves.at[y], gap_send, gap_recv, at(i, z, yo))
    gap_to.start()

    def raise_to(k):
        return send(outgoing.at[k], raises.at[here], raise_send.at[k], raise_recv.at[here],
                    at(k % GROUP, z, k // GROUP))

    for k in range(2 * GROUP):
        first = (k % GROUP) * own + (k // GROUP) * half
        column = jnp.max(top[first:first + half], axis=1, keepdims=True)
        shape = (half, LANES)
        row = jnp.max(jnp.where(iota(shape, 1) == iota(shape, 0), column, -jnp.inf), axis=0, keepdims=True)
        outgoing[k] = jnp.where(iota(row.shape, 1) == LANES - 1, bidders, row)

        @pl.when(here != k)
        def _():
            raise_to(k).start()

    raises[here] = outgoing[here]
    units = prices[i].astype(jnp.float32)
    own_prices = jnp.where(y == 0, units[:, :half], units[:, half:2 * half]) * unit_price

    arrived(halves.at[yo], gap_recv)
    both = jnp.concatenate([halves[0], halves[1]], axis=1)
    hit = where_to[...] == iota((2 * cap, own), 0).astype(jnp.float32)
    margins_out[...] = jnp.sum(jnp.where(hit, column_of(both, 2 * cap), 0.0), axis=0, keepdims=True)

    for ii, yy in plane:
        arrived(raises.at[yy * GROUP + ii], raise_recv.at[yy * GROUP + ii])
    highest, total = raises[0], raises[0]
    for k in range(1, 2 * GROUP):
        highest = jnp.maximum(highest, raises[k])
        total = total + raises[k]
    prices_out[...] = own_prices + jnp.maximum(highest[:, :half], 0.0)
    count_out[...] = (total[:, LANES - 1:] * 0.5).astype(jnp.int32)

    swap.wait_send()
    gap_to.wait_send()
    for copy in slot_sends + price_sends:
        copy.wait_send()
    loop(1, lines, lambda d: stat_to(d).wait_send())
    for k in range(2 * GROUP):
        @pl.when(here != k)
        def _():
            raise_to(k).wait_send()

    def passed(zb):
        @pl.when(has_right & (zb <= z))
        def _():
            to_right(0, zb).wait_send()
            to_right(1, zb).wait_send()

        @pl.when(has_left & (zb >= z))
        def _():
            to_left(0, zb).wait_send()
            to_left(1, zb).wait_send()

    loop(0, lines, passed)


def on_device(tokens, slot_embed, price_units, unassigned):
    lines = lax.axis_size("dp") // GROUP
    own, width = tokens.shape
    half, cap = own // 2, BUSY // 2
    every = GROUP * own
    any_ = pl.BlockSpec(memory_space=pl.ANY)
    vmem = pl.BlockSpec(memory_space=pltpu.VMEM)
    dma = pltpu.SemaphoreType.DMA
    new_prices, margins, total = pl.pallas_call(
        functools.partial(kernel, lines, cap),
        out_shape=(
            pltpu.VMEM((1, half), jnp.float32),
            pltpu.VMEM((1, own), jnp.float32),
            pltpu.VMEM((1, 1), jnp.int32),
        ),
        in_specs=[any_] * 4,
        out_specs=(vmem,) * 3,
        scratch_shapes=[
            pltpu.VMEM((2, GROUP, own, width), jnp.bfloat16),
            pltpu.VMEM((2, lines, cap, width), jnp.bfloat16),
            pltpu.VMEM((own, width), jnp.bfloat16),
            pltpu.VMEM((cap, width), jnp.bfloat16),
            pltpu.VMEM((GROUP, 1, own), jnp.int32),
            pltpu.VMEM((1, own), jnp.int32),
            pltpu.VMEM((1, own), jnp.float32),
            pltpu.VMEM((every, cap), jnp.float32),
            pltpu.VMEM((lines, 2 * lines, LANES), jnp.float32),
            pltpu.VMEM((2 * GROUP, 1, LANES), jnp.float32),
            pltpu.VMEM((2 * GROUP, 1, LANES), jnp.float32),
            pltpu.VMEM((lines, every, cap), jnp.float32),
            pltpu.VMEM((lines, 1, cap), jnp.float32),
            pltpu.VMEM((2, 1, cap), jnp.float32),
            dma((4,)), dma((7,)), dma((2, GROUP)), dma, dma((2, lines)), dma((2, lines)), dma((2, lines)),
            dma((3,)), dma((GROUP,)), dma((lines,)), dma((lines,)), dma((2 * GROUP,)), dma((2 * GROUP,)), dma, dma,
        ],
        compiler_params=pltpu.CompilerParams(collective_id=0, has_side_effects=True),
        name="auction",
    )(tokens, slot_embed, price_units.reshape(1, -1), unassigned.reshape(1, -1))
    return new_prices.reshape(-1), margins.reshape(-1), total.reshape(())


def solution(mesh):
    return jax.shard_map(
        on_device,
        mesh=mesh,
        in_specs=(P("dp", "mp"), P("dp", "mp"), P("dp"), P("dp")),
        out_specs=(P(("dp", "mp")), P("dp"), P()),
        check_vma=False,
    )
```

time: 34.3 us -> 30.6 us (0.89)
  Pallas kernels: 29.8 us -> 27.5 us
  local copies, waits for them, and re-layouts: 1.86 us -> 1.08 us
  between operations: 2.4 us -> 1.8 us
    pallas_call x1, Pallas kernels: 29.8 us -> 27.5 us  [on_device(): pl.pallas_call(functools.partial(kernel, lines, cap), out_shape=(pltpu.VM...]
    unnamed x6 -> x2, local copies, waits for them, and re-layouts: 1.86 us -> 1.08 us
where the time goes in v2:
time: 30.6 us; the launch traced here: 30.4 us
  Pallas kernels  27.5 us (90%)
  between operations  1.8 us (6%)
  local copies, waits for them, and re-layouts  1.08 us (4%)
    pallas_call x1, Pallas kernels, on_device(): pl.pallas_call(functools.partial(kernel, lines, cap), out_shape=(pltpu.VM...  27.5 us
    unnamed x2, local copies, waits for them, and re-layouts  1.08 us

profile of v2, /device:TPU:0, one launch (start us, length us, event | category | flops | bytes accessed | tf_op | source)
XLA Modules:
  0.0 30.4 jit_solution(3126406983802459219)
XLA Ops:
  0.6 27.5 %auction.1 = (f32[1,80]{1,0:T(1,128)S(1)}, f32[1,160]{1,0:T(1,128)S(1)}, s32[1,1]{1,0:T(1,128)S(1)}) custom-call(bf16[160,512]{1,0:T(8,128)(2,1)} %tok_in.1, bf16[160,512]{1,0:T(8,128)(2,1)} %slot_in.1, s32[1,160]{1,0:T(1,128)} %bitcast.7, s32[1,160]{1,0:T(1,128)} %bitcast.8), custom_call_target="tpu_custom_call" | custom-call | tf_op jit(solution)/shard_map/auction/pallas_call | solution.py:337
  28.2 0.5 %copy.10 = f32[80]{0:T(128)} copy(f32[80]{0:T(128)S(1)} %bitcast.6) | data formatting | bytes 640
  28.7 0.6 %copy.11 = f32[160]{0:T(256)} copy(f32[160]{0:T(256)S(1)} %bitcast.5) | data formatting | bytes 1280

commit v3 on v2

--- a/solution.py
+++ b/solution.py
@@ -114,34 +114,57 @@
     def _():
         pl.semaphore_wait(barrier, len(plane) + min(lines - 1, 1))
 
-    def to_right(f, zb):
-        return send(toks.at[f, zb], toks.at[f, zb], right_send.at[f, zb], tok_recv.at[f, zb],
-                    at(i, lax.rem(z + 1, lines), y))
-
-    def to_left(f, zb):
-        return send(toks.at[f, zb], toks.at[f, zb], left_send.at[f, zb], tok_recv.at[f, zb],
+    def to_right(f, zb, q):
+        block = tok_part(f, zb, q)
+        return send(block, block, right_send.at[f, zb, q], tok_recv.at[f, zb, q], at(i, lax.rem(z + 1, lines), y))
+
+    def to_left(f, zb, q):
+        block = tok_part(f, zb, q)
+        return send(block, block, left_send.at[f, zb, q], tok_recv.at[f, zb, q],
                     at(i, lax.rem(z + lines - 1, lines), y))
 
-    def send_both(f):
+    def tok_part(f, zb, q):
+        rows = toks.shape[2] // 2
+        return toks.at[f, zb, pl.ds(q * rows, rows)]
+
+    def slot_part(f, ii, q):
+        return slot.at[f, ii, pl.ds(q * half, half)]
+
+    def tok_arrived(f, zb, q):
+        arrived(tok_part(f, zb, q), tok_recv.at[f, zb, q])
+
+    def slot_arrived(f, ii, q):
+        arrived(slot_part(f, ii, q), slot_recv.at[f, ii, q])
+
+    def send_both(f, q):
         @pl.when(has_right)
         def _():
-            to_right(f, z).start()
+            to_right(f, z, q).start()
 
         @pl.when(has_left)
         def _():
-            to_left(f, z).start()
-
-    swap = send(spare, toks.at[y, z], swap_send, tok_recv.at[y, z], at(i, z, yo))
-    swap.start()
-    send_both(y)
+            to_left(f, z, q).start()
+
+    swaps = [
+        send(spare.at[pl.ds(q * (cap // 2), cap // 2)], tok_part(y, z, q), swap_send.at[q], tok_recv.at[y, z, q],
+             at(i, z, yo))
+        for q in range(2)
+    ]
+    for q in range(2):
+        swaps[q].start()
+        send_both(y, q)
+    slot_sends = []
+
+    def send_slots(f, ii, q, device):
+        block = slot_part(f, ii, q)
+        copy = send(block, block, slot_send.at[len(slot_sends)], slot_recv.at[f, ii, q], device)
+        copy.start()
+        slot_sends.append(copy)
+
     loads[2].wait()
-    mine = slot.at[y, i]
-    slot_sends = [
-        send(mine, mine, slot_send.at[k], slot_recv.at[y, i], device)
-        for k, device in enumerate([at(i2, z, y), at(i, z, yo), at(i1, z, y), at(i2, z, yo)])
-    ]
-    for copy in slot_sends:
-        copy.start()
+    for device in (at(i2, z, y), at(i, z, yo), at(i1, z, y)):
+        for q in range(2):
+            send_slots(y, i, q, device)
     loads[3].wait()
     price_sends = [
         send(prices.at[i], prices.at[i], price_send.at[k], price_recv.at[i], at(ii, z, y))
@@ -150,46 +173,60 @@
     for copy in price_sends:
         copy.start()
 
-    def relay(d, f):
+    def relay(d, f, q):
         @pl.when(has_right & (z - d >= 0))
         def _():
             zb = lax.max(z - d, 0)
-            arrived(toks.at[f, zb], tok_recv.at[f, zb])
-            to_right(f, zb).start()
+            tok_arrived(f, zb, q)
+            to_right(f, zb, q).start()
 
         @pl.when(has_left & (z + d < lines))
         def _():
             zb = lax.min(z + d, lines - 1)
-            arrived(toks.at[f, zb], tok_recv.at[f, zb])
-            to_left(f, zb).start()
-
-    def pass_on(f, ii, k):
-        block = slot.at[f, ii]
-        arrived(block, slot_recv.at[f, ii])
-        copy = send(block, block, slot_send.at[k], slot_recv.at[f, ii], at(i1, z, y))
-        copy.start()
-        slot_sends.append(copy)
-
-    arrived(toks.at[yo, z], tok_recv.at[yo, z])
-    send_both(yo)
-    relay(1, y)
-    pass_on(y, i2, 4)
-    relay(1, yo)
-    pass_on(yo, i, 5)
-    if lines > 2:
-        def relay_both(d):
-            relay(d, y)
-            relay(d, yo)
-
-        loop(2, lines - 1, relay_both)
+            tok_arrived(f, zb, q)
+            to_left(f, zb, q).start()
+
+    beside, across, over = at(i1, z, y), at(i2, z, y), at(i, z, yo)
+    for q in range(2):
+        tok_arrived(yo, z, q)
+        send_both(yo, q)
+        relay(1, y, q)
+    slot_arrived(y, i2, 0)
+    send_slots(y, i2, 0, beside)
+    relay(1, yo, 0)
+    slot_arrived(yo, i, 0)
+    send_slots(yo, i, 0, across)
+    send_slots(yo, i, 0, beside)
+    slot_arrived(y, i2, 1)
+    send_slots(y, i2, 1, over)
+    send_slots(y, i2, 1, beside)
+    relay(1, yo, 1)
+    if lines > 3:
+        for q in range(2):
+            relay(2, y, q)
+    slot_arrived(yo, i, 1)
+    send_slots(yo, i, 1, beside)
+    if lines > 3:
+        for q in range(2):
+            relay(2, yo, q)
+
+        def relay_all(d):
+            for f in (y, yo):
+                for q in range(2):
+                    relay(d, f, q)
+
+        loop(3, lines - 1, relay_all)
     for ii in (i1, i2, i3):
         arrived(prices.at[ii], price_recv.at[ii])
     for k in range(GROUP):
         column = column_of(prices[k].astype(jnp.float32) * unit_price, own)
         cost[k * own:(k + 1) * own] = jnp.broadcast_to(column, (own, cap))
-    pass_on(yo, i2, 6)
+    for q in range(2):
+        slot_arrived(yo, i2, q)
+        send_slots(yo, i2, q, beside)
     for f, ii in [(y, i1), (y, i3), (yo, i1), (yo, i3)]:
-        arrived(slot.at[f, ii], slot_recv.at[f, ii])
+        for q in range(2):
+            slot_arrived(f, ii, q)
 
     def score(zb):
         total = None
@@ -223,8 +260,9 @@
 
             @pl.when(jnp.logical_not(has_right))
             def _():
-                arrived(toks.at[y, zb], tok_recv.at[y, zb])
-                arrived(toks.at[yo, zb], tok_recv.at[yo, zb])
+                for q in range(2):
+                    tok_arrived(y, zb, q)
+                    tok_arrived(yo, zb, q)
 
             score(zb)
 
@@ -234,8 +272,9 @@
 
             @pl.when(jnp.logical_not(has_left))
             def _():
-                arrived(toks.at[y, zb], tok_recv.at[y, zb])
-                arrived(toks.at[yo, zb], tok_recv.at[yo, zb])
+                for q in range(2):
+                    tok_arrived(y, zb, q)
+                    tok_arrived(yo, zb, q)
 
             score(zb)
 
@@ -302,9 +341,8 @@
     prices_out[...] = own_prices + jnp.maximum(highest[:, :half], 0.0)
     count_out[...] = (total[:, LANES - 1:] * 0.5).astype(jnp.int32)
 
-    swap.wait_send()
     gap_to.wait_send()
-    for copy in slot_sends + price_sends:
+    for copy in swaps + slot_sends + price_sends:
         copy.wait_send()
     loop(1, lines, lambda d: stat_to(d).wait_send())
     for k in range(2 * GROUP):
@@ -312,16 +350,18 @@
         def _():
             raise_to(k).wait_send()
 
+    pieces = [(f, q) for f in range(2) for q in range(2)]
+
     def passed(zb):
         @pl.when(has_right & (zb <= z))
         def _():
-            to_right(0, zb).wait_send()
-            to_right(1, zb).wait_send()
+            for f, q in pieces:
+                to_right(f, zb, q).wait_send()
 
         @pl.when(has_left & (zb >= z))
         def _():
-            to_left(0, zb).wait_send()
-            to_left(1, zb).wait_send()
+            for f, q in pieces:
+                to_left(f, zb, q).wait_send()
 
     loop(0, lines, passed)
 
@@ -358,7 +398,8 @@
             pltpu.VMEM((lines, every, cap), jnp.float32),
             pltpu.VMEM((lines, 1, cap), jnp.float32),
             pltpu.VMEM((2, 1, cap), jnp.float32),
-            dma((4,)), dma((7,)), dma((2, GROUP)), dma, dma((2, lines)), dma((2, lines)), dma((2, lines)),
+            dma((4,)), dma((14,)), dma((2, GROUP, 2)), dma((2,)), dma((2, lines, 2)), dma((2, lines, 2)),
+            dma((2, lines, 2)),
             dma((3,)), dma((GROUP,)), dma((lines,)), dma((lines,)), dma((2 * GROUP,)), dma((2 * GROUP,)), dma, dma,
         ],
         compiler_params=pltpu.CompilerParams(collective_id=0, has_side_effects=True),

time: 30.6 us -> 28.4 us (0.928)
  Pallas kernels: 27.5 us -> 25.4 us
    pallas_call x1, Pallas kernels: 27.5 us -> 25.4 us  [on_device(): pl.pallas_call(functools.partial(kernel, lines, cap), out_shape=(pltpu.VM...]
where the time goes in v3:
time: 28.4 us; the launch traced here: 28.2 us
  Pallas kernels  25.4 us (89%)
  between operations  1.8 us (6%)
  local copies, waits for them, and re-layouts  1.08 us (4%)
    pallas_call x1, Pallas kernels, on_device(): pl.pallas_call(functools.partial(kernel, lines, cap), out_shape=(pltpu.VM...  25.4 us
    unnamed x2, local copies, waits for them, and re-layouts  1.08 us

profile of v3, /device:TPU:0, one launch (start us, length us, event | category | flops | bytes accessed | tf_op | source)
XLA Modules:
  0.0 28.2 jit_solution(13931794811461470511)
XLA Ops:
  0.6 25.4 %auction.1 = (f32[1,80]{1,0:T(1,128)S(1)}, f32[1,160]{1,0:T(1,128)S(1)}, s32[1,1]{1,0:T(1,128)S(1)}) custom-call(bf16[160,512]{1,0:T(8,128)(2,1)} %tok_in.1, bf16[160,512]{1,0:T(8,128)(2,1)} %slot_in.1, s32[1,160]{1,0:T(1,128)} %bitcast.7, s32[1,160]{1,0:T(1,128)} %bitcast.8), custom_call_target="tpu_custom_call" | custom-call | tf_op jit(solution)/shard_map/auction/pallas_call | solution.py:377
  26.0 0.5 %copy.10 = f32[80]{0:T(128)} copy(f32[80]{0:T(128)S(1)} %bitcast.6) | data formatting | bytes 640
  26.5 0.6 %copy.11 = f32[160]{0:T(256)} copy(f32[160]{0:T(256)S(1)} %bitcast.5) | data formatting | bytes 1280

commit v4 on v3

--- a/solution.py
+++ b/solution.py
@@ -228,9 +228,15 @@
         for q in range(2):
             slot_arrived(f, ii, q)
 
-    def score(zb):
+    def score(zb, late=None):
         total = None
-        for f in range(2):
+        for f in (y, yo):
+            if late is not None:
+                @pl.when(late)
+                def _():
+                    for q in range(2):
+                        tok_arrived(f, zb, q)
+
             rows = slot[f].reshape(GROUP * own, slot.shape[3])
             part = lax.dot_general(
                 rows, toks[f, zb], (((1,), (1,)), ((), ())), preferred_element_type=jnp.float32
@@ -258,25 +264,13 @@
         def _():
             zb = lax.max(z - d, 0)
 
-            @pl.when(jnp.logical_not(has_right))
-            def _():
-                for q in range(2):
-                    tok_arrived(y, zb, q)
-                    tok_arrived(yo, zb, q)
-
-            score(zb)
+            score(zb, jnp.logical_not(has_right))
 
         @pl.when(z + d < lines)
         def _():
             zb = lax.min(z + d, lines - 1)
 
-            @pl.when(jnp.logical_not(has_left))
-            def _():
-                for q in range(2):
-                    tok_arrived(y, zb, q)
-                    tok_arrived(yo, zb, q)
-
-            score(zb)
+            score(zb, jnp.logical_not(has_left))
 
     stats[z, lines:] = jnp.broadcast_to(busy, (lines, LANES))
     loop(1, lines, score_at)

time: 28.4 us -> 28.4 us (level)
  no operation moved by 1% of the time
where the time goes in v4:
time: 28.4 us; the launch traced here: 28.2 us
  Pallas kernels  25.4 us (89%)
  between operations  1.8 us (6%)
  local copies, waits for them, and re-layouts  1.08 us (4%)
    pallas_call x1, Pallas kernels, on_device(): pl.pallas_call(functools.partial(kernel, lines, cap), out_shape=(pltpu.VM...  25.4 us
    unnamed x2, local copies, waits for them, and re-layouts  1.08 us

profile of v4, /device:TPU:0, one launch (start us, length us, event | category | flops | bytes accessed | tf_op | source)
XLA Modules:
  0.0 28.2 jit_solution(12561957682160985132)
XLA Ops:
  0.6 25.4 %auction.1 = (f32[1,80]{1,0:T(1,128)S(1)}, f32[1,160]{1,0:T(1,128)S(1)}, s32[1,1]{1,0:T(1,128)S(1)}) custom-call(bf16[160,512]{1,0:T(8,128)(2,1)} %tok_in.1, bf16[160,512]{1,0:T(8,128)(2,1)} %slot_in.1, s32[1,160]{1,0:T(1,128)} %bitcast.7, s32[1,160]{1,0:T(1,128)} %bitcast.8), custom_call_target="tpu_custom_call" | custom-call | tf_op jit(solution)/shard_map/auction/pallas_call | solution.py:371
  26.0 0.5 %copy.10 = f32[80]{0:T(128)} copy(f32[80]{0:T(128)S(1)} %bitcast.6) | data formatting | bytes 640
  26.5 0.6 %copy.11 = f32[160]{0:T(256)} copy(f32[160]{0:T(256)S(1)} %bitcast.5) | data formatting | bytes 1280
